TPU v7x, 32 devices: a whole 2x2x4 slice. The times are simulated.
32 devices in a mesh: groups: 2 (over y), chan: 8 (over z, x), sub: 2 (over core).
Axes of the slice: x: 2, y: 2, z: 4, core: 2. Of those that a mesh axis runs over, the one named last changes fastest.
Arguments:
- predicted_sky_response: bfloat16 [16384, 8, 2, 128], P(('groups', 'chan', 'sub')), parts along dimension 0, may hold values from -0.4375 to 0.4375
- measured_correlation: bfloat16 [16384, 2, 128], P(('groups', 'chan', 'sub')), parts along dimension 0, may hold values from -6 to 6
- keep_indicator: int32 [16384, 128], P(('groups', 'chan', 'sub')), parts along dimension 0, may hold values 0 or 1
- tile_owner: int32 [16384, 1], P(('groups', 'chan', 'sub')), parts along dimension 0, may hold values from 0 to 7; in each aligned block of 512 rows (0 to 511, 512 to 1023, ...) at most 192 rows name the same one
- tile_channel: int32 [16384], P(('groups', 'chan', 'sub')), parts along dimension 0, may hold values from 0 to 3
- tile_base: int32 [16384], P(('groups', 'chan', 'sub')), parts along dimension 0, may hold values from 0 to 14
- pairs: int32 [15, 2, 128], replicated, may hold values from 0 to 61, as said below
- gains: float32 [64, 2, 62, 8], P(('groups', 'chan')), parts along dimension 0, may hold values from -5 to 5
- duals: float32 [64, 2, 62, 8], P(('groups', 'chan', 'sub')), parts along dimension 0, may hold values from -4 to 4
- consensus: float32 [8, 2, 62, 8], P('groups'), parts along dimension 0, may hold values from -5 to 5
- rho: float32 [8], replicated, may hold values from 0.3 to 3
Outputs:
- gains_new: float32 [64, 2, 62, 8], P(('groups', 'chan', 'sub')), parts along dimension 0
- consensus_new: float32 [8, 2, 62, 8], P('groups'), parts along dimension 0
- duals_new: float32 [64, 2, 62, 8], P(('groups', 'chan', 'sub')), parts along dimension 0
There are 2 independent parts, one for each index of `groups`. A program takes and returns all parts, laid end to end along the dimension named above; an argument that names none is the same for every part. Nothing has to cross between parts.
Inputs may be any that keep to these rules, and one draw needn't show every extreme that they name: `tile_owner`: on the tiles of one device at most 192 name the same owner, a bound that some block reaches. `pairs`: the two stations of a row differ.
All inputs are finite; a program needn't handle non-finite values. No bound on the sum of `keep_indicator` on one device may be relied on, other than what follows from the above.
Results may differ from a plain program's by a relative error of at most 0.0027.
Values may be sent and summed in bfloat16 or wider, within the bound.
A program may use at most 128 MiB of HBM per device.

v0:
```python
import math
import jax
import jax.numpy as jnp
from jax import lax
from jax.sharding import PartitionSpec as P


def legendre_rows(channels):
    positions = jnp.arange(channels, dtype=jnp.float32)
    abscissa = (2.0 * positions - (channels - 1)) / max(channels - 1, 1)
    return jnp.stack(
        [
            jnp.ones_like(abscissa),
            abscissa,
            0.5 * (3.0 * abscissa * abscissa - 1.0),
            0.5 * (5.0 * abscissa * abscissa * abscissa - 3.0 * abscissa),
        ]
    )


def outer_terms(vector_real, vector_imag, weight_real, weight_imag):
    tiles_count, row_total_count, directions = vector_real.shape
    outer_real = (
        vector_real[..., :, None] * vector_real[..., None, :]
        + vector_imag[..., :, None] * vector_imag[..., None, :]
    )
    outer_imag = (
        vector_real[..., :, None] * vector_imag[..., None, :]
        - vector_imag[..., :, None] * vector_real[..., None, :]
    )
    normal = jnp.stack([outer_real, outer_imag], axis=2).reshape(
        tiles_count, row_total_count, 2 * directions * directions
    )
    side_real = vector_real * weight_real[..., None] + vector_imag * weight_imag[..., None]
    side_imag = vector_real * weight_imag[..., None] - vector_imag * weight_real[..., None]
    right_side = jnp.stack([side_real, side_imag], axis=2).reshape(
        tiles_count, row_total_count, 2 * directions
    )
    return (normal, right_side)


def row_terms(coupling, observed, near_gain, far_gain):
    coupling_real = jnp.swapaxes(coupling[:, :, 0, :], 1, 2).astype(jnp.float32)
    coupling_imag = jnp.swapaxes(coupling[:, :, 1, :], 1, 2).astype(jnp.float32)
    near_real, near_imag = (near_gain[:, :, 0, :], near_gain[:, :, 1, :])
    far_real, far_imag = (far_gain[:, :, 0, :], far_gain[:, :, 1, :])
    slope_real = coupling_real * far_real + coupling_imag * far_imag
    slope_imag = coupling_imag * far_real - coupling_real * far_imag
    mirror_real = coupling_real * near_real - coupling_imag * near_imag
    mirror_imag = -(coupling_real * near_imag + coupling_imag * near_real)
    model_real = jnp.sum(near_real * slope_real - near_imag * slope_imag, axis=-1)
    model_imag = jnp.sum(near_real * slope_imag + near_imag * slope_real, axis=-1)
    observed_f = observed.astype(jnp.float32)
    residual_real = observed_f[:, 0, :] - model_real
    residual_imag = observed_f[:, 1, :] - model_imag
    normal_near, right_near = outer_terms(slope_real, slope_imag, residual_real, residual_imag)
    normal_far, right_far = outer_terms(mirror_real, mirror_imag, residual_real, -residual_imag)
    normal = jnp.concatenate([normal_near, normal_far], axis=1).astype(jnp.bfloat16)
    right_side = jnp.concatenate([right_near, right_far], axis=1).astype(jnp.bfloat16)
    return (normal, right_side)


def tile_normals(coupling, observed, channel_index, base_index, pairs, gain_table):
    stations_count = gain_table.shape[2]
    stations = pairs[base_index]
    station_ids = jnp.arange(stations_count, dtype=jnp.int32)
    near_onehot = (stations[:, 0, :, None] == station_ids).astype(jnp.float32)
    far_onehot = (stations[:, 1, :, None] == station_ids).astype(jnp.float32)
    tile_gains = gain_table[channel_index]
    near_gain = jnp.einsum(
        "trs,tcsk->trck", near_onehot, tile_gains, precision=lax.Precision.HIGHEST
    )
    far_gain = jnp.einsum("trs,tcsk->trck", far_onehot, tile_gains, precision=lax.Precision.HIGHEST)
    normal, right_side = row_terms(coupling, observed, near_gain, far_gain)
    both_onehot = jnp.concatenate([near_onehot, far_onehot], axis=1).astype(jnp.bfloat16)
    tile_normal = jnp.einsum(
        "trs,trc->tsc", both_onehot, normal, preferred_element_type=jnp.float32
    )
    tile_right = jnp.einsum(
        "trs,trc->tsc", both_onehot, right_side, preferred_element_type=jnp.float32
    )
    return (tile_normal, tile_right)


def accumulate(coupling, observed, channel_index, base_index, pairs, gain_table, channel_slots):
    tiles_count = coupling.shape[0]
    block_size = math.gcd(tiles_count, 32)
    iteration_tally = tiles_count // block_size
    stations_count = gain_table.shape[2]
    directions = gain_table.shape[3]

    def one_step(totals, block_item):
        normal_acc, right_acc = totals
        tile_normal, tile_right = tile_normals(
            block_item[0], block_item[1], block_item[2], block_item[3], pairs, gain_table
        )
        return (
            (
                normal_acc.at[block_item[2]].add(tile_normal),
                right_acc.at[block_item[2]].add(tile_right),
            ),
            None,
        )

    block_items = (
        coupling.reshape((iteration_tally, block_size) + coupling.shape[1:]),
        observed.reshape((iteration_tally, block_size) + observed.shape[1:]),
        channel_index.reshape(iteration_tally, block_size),
        base_index.reshape(iteration_tally, block_size),
    )
    start_totals = (
        jnp.zeros((channel_slots, stations_count, 2 * directions * directions), jnp.float32),
        jnp.zeros((channel_slots, stations_count, 2 * directions), jnp.float32),
    )
    (normal_sum, right_sum), _ = lax.scan(one_step, start_totals, block_items)
    return (normal_sum, right_sum)


def admm_update(normal, right_side, gain, dual, anchor, rho):
    count, stations = (normal.shape[0], normal.shape[1])
    directions = rho.shape[0]
    normal_blocks = normal.reshape(count, stations, 2, directions, directions)
    ridge_diag = jnp.diag(rho)
    higher_half_records = jnp.concatenate(
        [normal_blocks[:, :, 0] + ridge_diag, -normal_blocks[:, :, 1]], axis=-1
    )
    lower_rows = jnp.concatenate(
        [normal_blocks[:, :, 1], normal_blocks[:, :, 0] + ridge_diag], axis=-1
    )
    system = jnp.concatenate([higher_half_records, lower_rows], axis=-2)
    gain_rows = jnp.transpose(gain, (0, 2, 1, 3))
    dual_rows = jnp.transpose(dual, (0, 2, 1, 3))
    anchor_rows = jnp.transpose(anchor, (0, 2, 1, 3))
    target = (
        right_side.reshape(count, stations, 2, directions)
        - dual_rows
        - rho * (gain_rows - anchor_rows)
    )
    factor = jnp.linalg.cholesky(system)
    gain_step = jax.scipy.linalg.cho_solve(
        (factor, True), target.reshape(count, stations, 2 * directions)[..., None]
    )[..., 0]
    return gain + jnp.transpose(gain_step.reshape(count, stations, 2, directions), (0, 2, 1, 3))


def fit_consensus(poly_basis, summed):
    gram_matrix = jnp.dot(poly_basis, poly_basis.T, precision=lax.Precision.HIGHEST)
    factor = jnp.linalg.cholesky(gram_matrix)
    coeffs = jax.scipy.linalg.cho_solve((factor, True), summed.reshape(summed.shape[0], -1))
    return coeffs.reshape(summed.shape)


def body(
    predicted_sky_response,
    measured_correlation,
    keep_indicator,
    tile_owner,
    tile_channel,
    tile_base,
    pairs,
    gains,
    duals,
    consensus,
    rho,
):
    channels_here = gains.shape[0]
    chan_count = lax.axis_size("chan")
    sub_count = lax.axis_size("sub")
    half_count = channels_here // sub_count
    retained_selector = keep_indicator > 0
    predicted_response_kept = jnp.where(
        retained_selector[:, None, None, :],
        predicted_sky_response,
        jnp.zeros_like(predicted_sky_response),
    )
    measured_correlation_kept = jnp.where(
        retained_selector[:, None, :], measured_correlation, jnp.zeros_like(measured_correlation)
    )
    owner_index = tile_owner[:, 0]
    all_gains = lax.all_gather(gains, "chan", axis=0, tiled=True)
    full_channel = owner_index * channels_here + tile_channel
    normal_sum, right_sum = accumulate(
        predicted_response_kept,
        measured_correlation_kept,
        full_channel,
        tile_base,
        pairs,
        all_gains,
        channels_here * chan_count,
    )
    normal_part, right_part = (
        lax.psum_scatter(normal_sum, ("chan", "sub"), scatter_dimension=0, tiled=True),
        lax.psum_scatter(right_sum, ("chan", "sub"), scatter_dimension=0, tiled=True),
    )
    sub_index = lax.axis_index("sub")
    chan_index = lax.axis_index("chan")
    my_gains = lax.dynamic_slice_in_dim(gains, sub_index * half_count, half_count, 0)
    poly_basis = legendre_rows(channels_here * chan_count)
    first_channel = (chan_index * sub_count + sub_index) * half_count
    my_basis = lax.dynamic_slice_in_dim(poly_basis, first_channel, half_count, 1)
    anchor = jnp.einsum("df,dcsk->fcsk", my_basis, consensus, precision=lax.Precision.HIGHEST)
    gains_new = admm_update(normal_part, right_part, my_gains, duals, anchor, rho)
    partial_value = jnp.einsum(
        "df,fcsk->dcsk", my_basis, gains_new + duals / rho, precision=lax.Precision.HIGHEST
    )
    summed = lax.psum(partial_value, ("chan", "sub"))
    consensus_new = fit_consensus(poly_basis, summed)
    duals_new = duals + rho * (
        gains_new
        - jnp.einsum("df,dcsk->fcsk", my_basis, consensus_new, precision=lax.Precision.HIGHEST)
    )
    return (gains_new, consensus_new, duals_new)


def solution(mesh):
    placed = (
        P(("groups", "chan", "sub"), None, None, None),
        P(("groups", "chan", "sub"), None, None),
        P(("groups", "chan", "sub"), None),
        P(("groups", "chan", "sub"), None),
        P(("groups", "chan", "sub")),
        P(("groups", "chan", "sub")),
        P(),
        P(("groups", "chan"), None, None, None),
        P(("groups", "chan", "sub"), None, None, None),
        P("groups", None, None, None),
        P(),
    )
    return jax.shard_map(
        body,
        mesh=mesh,
        in_specs=placed,
        out_specs=(
            P(("groups", "chan", "sub"), None, None, None),
            P("groups", None, None, None),
            P(("groups", "chan", "sub"), None, None, None),
        ),
        check_vma=False,
    )
```

profile of v0, /device:TPU:0, one launch (start us, length us, event | category | flops | bytes accessed | tf_op | source)
XLA Modules:
  0.0 650.6 jit_solution(18375419178991925934)
XLA Ops:
  8.3 3.6 copy_select_fusion
  12.0 32.6 %all_gather.3 = f32[32,2,62,8]{2,3,1,0:T(8,128)S(1)} all-gather(f32[4,2,62,8]{2,3,1,0:T(8,128)S(1)} %copy-done.8), channel_id=1, replica_groups=mesh['groups'=2,'chan'=8,'sub'=2] {'chan'}, dimensions={0}, use_global_device_ids=true | all-gather | bytes 142848 | tf_op jit(solution)/shard_map/all_gather | solution.py:180
  44.9 225.0 %while.12 = (s32[]{:T(128)}, f32[32,62,128]{2,1,0:T(8,128)S(1)}, f32[32,62,16]{1,2,0:T(8,128)S(1)}, s32[16,32]{1,0:T(8,128)S(1)}, s32[16,32]{1,0:T(8,128)S(1)}, ...) while((s32[]{:T(128)}, f32[32,62,128]{2,1,0:T(8,128)S(1)}, ...), condition=%wide.region_5.6_spmd, body=%wide.region_0.5_spmd.sunk | while | flops 259593408 | bytes 28256220 | solution.py:115
  49.5 1.8 scatter_fusion.1
  51.7 1.3 copy.187
  54.8 2.0 fusion.100
  56.8 2.1 scatter_fusion
  63.5 1.8 scatter_fusion.1
  65.7 1.3 copy.187
  68.8 2.0 fusion.100
  70.8 2.1 scatter_fusion
  77.6 1.7 scatter_fusion.1
  79.8 1.3 copy.187
  82.9 2.0 fusion.100
  84.9 2.1 scatter_fusion
  91.7 1.7 scatter_fusion.1
  93.8 1.3 copy.187
  96.9 2.0 fusion.100
  98.9 2.1 scatter_fusion
  105.7 1.7 scatter_fusion.1
  107.9 1.3 copy.187
  111.0 2.0 fusion.100
  113.0 2.1 scatter_fusion
  119.8 1.8 scatter_fusion.1
  122.0 1.3 copy.187
  125.1 2.0 fusion.100
  127.1 2.1 scatter_fusion
  133.8 1.7 scatter_fusion.1
  136.0 1.3 copy.187
  139.1 2.0 fusion.100
  141.1 2.1 scatter_fusion
  147.9 1.7 scatter_fusion.1
  153.2 2.0 fusion.100
  155.2 2.1 scatter_fusion
  161.9 1.7 scatter_fusion.1
  167.2 2.0 fusion.100
  169.2 2.1 scatter_fusion
  176.0 1.8 scatter_fusion.1
  181.3 2.0 fusion.100
  183.3 2.1 scatter_fusion
  190.1 1.8 scatter_fusion.1
  195.4 2.0 fusion.100
  197.4 2.1 scatter_fusion
  204.1 1.7 scatter_fusion.1
  209.4 2.0 fusion.100
  211.4 2.1 scatter_fusion
  218.2 1.7 scatter_fusion.1
  223.5 2.0 fusion.100
  225.5 2.1 scatter_fusion
  232.2 1.8 scatter_fusion.1
  237.5 2.0 fusion.100
  239.5 2.1 scatter_fusion
  246.3 1.8 scatter_fusion.1
  251.6 2.0 fusion.100
  253.6 2.1 scatter_fusion
  260.4 1.7 scatter_fusion.1
  265.7 2.0 fusion.100
  267.7 2.1 scatter_fusion
  270.6 2.0 copy.113
  275.2 52.2 %reduce-scatter.5.cloned.1.call-done = f32[2,62,16]{1,2,0:T(8,128)} async-done(((f32[32,62,16]{1,2,0:T(8,128)}), f32[2,62,16]{1,2,0:T(8,128)}) %reduce-scatter.5.cloned.1.call-update) | async-done | bytes 7952 | tf_op jit(solution)/shard_map/reduce_scatter | solution.py:193
  328.5 63.5 %reduce-scatter.3.cloned.1.call-done = f32[2,62,128]{1,2,0:T(8,128)} async-done(((f32[32,62,128]{1,2,0:T(8,128)}), f32[2,62,128]{1,2,0:T(8,128)}) %reduce-scatter.3.cloned.1.call-update) | async-done | bytes 63504 | tf_op jit(solution)/shard_map/reduce_scatter | solution.py:192
  394.5 181.8 %custom-call.21 = f32[2,62,16,16]{3,2,1,0:T(8,128)S(1)} custom-call(f32[2,62,16,16]{3,2,1,0:T(8,128)S(1)} %broadcast_multiply_fusion), custom_call_target="Cholesky" | custom-call | tf_op jit(solution)/shard_map/jit(cholesky)/cholesky | solution.py:139
  577.0 5.4 custom-call.22
  583.5 57.6 %psum.7 = f32[2,62,8,4]{1,3,2,0:T(4,128)S(1)} all-reduce(f32[2,62,8,4]{1,3,2,0:T(4,128)S(1)} %copy.126), channel_id=1, replica_groups=mesh['groups'=2,'chan'=8,'sub'=2] {'chan','sub'}, use_global_device_ids=true, to_apply=%region_12.13 | all-reduce | flops 3968 | bytes 31744 | tf_op jit(solution)/shard_map/psum | solution.py:206
  (597 shorter events, 130.8 us)
Async XLA Ops:
  7.2 320.9 %copy-start = (f32[4,2,62,8]{2,3,1,0:T(8,128)S(1)}, f32[4,2,62,8]{2,3,1,0:T(8,128)}, u32[]{:S(2)}) copy-start(f32[4,2,62,8]{2,3,1,0:T(8,128)} %param.22) | copy-start | bytes 47620
  7.2 320.2 %reduce-scatter.5.cloned.1.call-start = ((), (), s32[]{:S(2)}) async-start(), calls=%async_computation.3 | async-start | bytes 278528 | tf_op jit(solution)/shard_map/reduce_scatter | solution.py:193
  8.2 3.7 copy-start.7
  8.2 3.7 copy-start.8
  8.2 36.3 %copy-start.11 = (s32[512,1]{0,1:T(1,128)S(1)}, s32[512,1]{0,1:T(1,128)}, u32[]{:S(2)}) copy-start(s32[512,1]{0,1:T(1,128)} %param.16) | copy-start | bytes 6148
  8.3 36.3 %copy-start.9 = (s32[512]{0:T(512)S(1)}, s32[512]{0:T(512)}, u32[]{:S(2)}) copy-start(s32[512]{0:T(512)} %param.17) | copy-start | bytes 6148
  8.3 36.4 %copy-start.10 = (s32[512]{0:T(512)S(1)}, s32[512]{0:T(512)}, u32[]{:S(2)}) copy-start(s32[512]{0:T(512)} %param.18) | copy-start | bytes 6148
  11.9 33.0 %copy-start.4 = (s32[15,2,128]{2,1,0:T(2,128)S(1)}, s32[15,2,128]{2,1,0:T(2,128)}, u32[]{:S(2)}) copy-start(s32[15,2,128]{2,1,0:T(2,128)} %param.19) | copy-start | bytes 46084
  44.9 3.7 copy-start.5
  49.1 2.1 copy-start.2
  53.3 1.5 copy-start.3
  56.8 2.2 copy-start.6
  58.9 3.7 copy-start.5
  63.2 2.1 copy-start.2
  70.8 2.2 copy-start.6
  73.0 3.7 copy-start.5
  77.2 2.1 copy-start.2
  84.9 2.1 copy-start.6
  87.0 3.7 copy-start.5
  91.3 2.1 copy-start.2
  98.9 2.1 copy-start.6
  101.1 3.7 copy-start.5
  105.3 2.1 copy-start.2
  109.5 1.5 copy-start.3
  113.0 2.2 copy-start.6
  115.2 3.7 copy-start.5
  119.4 2.1 copy-start.2
  123.6 1.5 copy-start.3
  127.0 2.2 copy-start.6
  129.2 3.7 copy-start.5
  133.5 2.1 copy-start.2
  141.1 2.2 copy-start.6
  143.3 3.7 copy-start.5
  147.5 2.1 copy-start.2
  155.2 2.2 copy-start.6
  157.3 3.7 copy-start.5
  161.6 2.1 copy-start.2
  169.2 2.2 copy-start.6
  171.4 3.7 copy-start.5
  175.6 2.1 copy-start.2
  179.8 1.5 copy-start.3
  183.3 2.2 copy-start.6
  185.5 3.7 copy-start.5
  189.7 2.1 copy-start.2
  197.3 2.2 copy-start.6
  199.5 3.7 copy-start.5
  203.8 2.1 copy-start.2
  211.4 2.2 copy-start.6
  213.6 3.7 copy-start.5
  217.8 2.1 copy-start.2
  225.5 2.1 copy-start.6
  227.6 3.7 copy-start.5
  231.9 2.1 copy-start.2
  239.5 2.2 copy-start.6
  241.7 3.7 copy-start.5
  245.9 2.1 copy-start.2
  253.6 2.2 copy-start.6
  255.8 3.7 copy-start.5
  260.0 2.1 copy-start.2
  264.2 1.5 copy-start.3
  267.7 2.2 copy-start.6
  270.6 121.4 %reduce-scatter.3.cloned.1.call-start = ((), (), s32[]{:S(2)}) async-start(), calls=%async_computation.2 | async-start | bytes 2228224 | tf_op jit(solution)/shard_map/reduce_scatter | solution.py:192
  270.6 4.5 copy-start.12
  270.6 57.5 %copy-start.13 = (f32[2,2,62,8]{2,3,1,0:T(8,128)S(1)}, f32[2,2,62,8]{2,3,1,0:T(8,128)}, u32[]{:S(2)}) copy-start(f32[2,2,62,8]{2,3,1,0:T(8,128)} %param.21) | copy-start | bytes 23812
  (12 other events, 16.7 us)
Sparse Core Ops, SparseCore 0:
  270.7 56.6 reduce-scatter.4
  331.1 60.8 reduce-scatter.2
where the time goes:
time: 652 us; the launch traced here: 651 us
  other arithmetic  281 us (43%)
  waiting for transfers between devices  116 us (18%)
  blocking collectives  90.2 us (14%)
  local copies, waits for them, and re-layouts  85.5 us (13%)
  matrix products  59.6 us (9%)
  between operations  14.4 us (2%)
    another operation x4, other arithmetic, admm_update(): factor = jnp.linalg.cholesky(system)  182 us
    reduce_scatter x1, waiting for transfers between devices, body(): lax.psum_scatter(normal_sum, ('chan', 'sub'), scatter_dimension=0, tiled=...  63.5 us
    psum x1, blocking collectives, body(): summed = lax.psum(partial_value, ('chan', 'sub'))  57.6 us
    reduce_scatter x1, waiting for transfers between devices, body(): lax.psum_scatter(right_sum, ('chan', 'sub'), scatter_dimension=0, tiled=T...  52.2 us
    reshape x32, local copies, waits for them, and re-layouts, outer_terms(): jnp.stack([outer_real, outer_imag], axis=2)  42.6 us
    scatter-add x16, other arithmetic, one_step(): normal_acc.at[block_item[2]].add(tile_normal)  34.1 us
    all_gather x1, blocking collectives, body(): all_gains = lax.all_gather(gains, 'chan', axis=0, tiled=True)  32.6 us
    dot_general x16, matrix products, tile_normals(): jnp.einsum('trs,trc->tsc', both_onehot, normal, preferred_element_type=jn...  31.6 us
  transfers between devices with their start and end apart: 2, of which 2 were waited for; matrix products, arithmetic and copies ran while one was open for 1% of the time, Pallas kernels for 0%

commit v1 on v0

--- a/solution.py
+++ b/solution.py
@@ -203,7 +203,8 @@
     partial_value = jnp.einsum(
         "df,fcsk->dcsk", my_basis, gains_new + duals / rho, precision=lax.Precision.HIGHEST
     )
-    summed = lax.psum(partial_value, ("chan", "sub"))
+    parts = lax.all_gather(partial_value, ("chan", "sub"), axis=0, tiled=False)
+    summed = parts.sum(axis=0)
     consensus_new = fit_consensus(poly_basis, summed)
     duals_new = duals + rho * (
         gains_new

time: 652 us -> 615 us (0.943)
  blocking collectives: 90.2 us -> 53.3 us
    psum x1 -> x0, blocking collectives: 57.6 us -> none  [body(): summed = lax.psum(partial_value, ('chan', 'sub'))]
    all_gather x0 -> x1, blocking collectives: none -> 20.7 us  [body(): parts = lax.all_gather(partial_value, ('chan', 'sub'), axis=0, tiled=False)]
where the time goes in v1:
time: 615 us; the launch traced here: 614 us
  other arithmetic  281 us (46%)
  waiting for transfers between devices  116 us (19%)
  local copies, waits for them, and re-layouts  85.5 us (14%)
  matrix products  59.7 us (10%)
  blocking collectives  53.3 us (9%)
  between operations  14.4 us (2%)
    another operation x4, other arithmetic, admm_update(): factor = jnp.linalg.cholesky(system)  182 us
    reduce_scatter x1, waiting for transfers between devices, body(): lax.psum_scatter(normal_sum, ('chan', 'sub'), scatter_dimension=0, tiled=...  63.5 us
    reduce_scatter x1, waiting for transfers between devices, body(): lax.psum_scatter(right_sum, ('chan', 'sub'), scatter_dimension=0, tiled=T...  52.2 us
    reshape x32, local copies, waits for them, and re-layouts, outer_terms(): jnp.stack([outer_real, outer_imag], axis=2)  42.6 us
    scatter-add x16, other arithmetic, one_step(): normal_acc.at[block_item[2]].add(tile_normal)  34.1 us
    all_gather x1, blocking collectives, body(): all_gains = lax.all_gather(gains, 'chan', axis=0, tiled=True)  32.6 us
    dot_general x16, matrix products, tile_normals(): jnp.einsum('trs,trc->tsc', both_onehot, normal, preferred_element_type=jn...  31.6 us
    scatter-add x16, other arithmetic, one_step(): right_acc.at[block_item[2]].add(tile_right)  27.9 us
  transfers between devices with their start and end apart: 2, of which 2 were waited for; matrix products, arithmetic and copies ran while one was open for 1% of the time, Pallas kernels for 0%

profile of v1, /device:TPU:0, one launch (start us, length us, event | category | flops | bytes accessed | tf_op | source)
XLA Modules:
  0.0 613.8 jit_solution(2138049456885429738)
XLA Ops:
  8.3 3.6 copy_select_fusion
  12.0 32.6 %all_gather.9 = f32[32,2,62,8]{2,3,1,0:T(8,128)S(1)} all-gather(f32[4,2,62,8]{2,3,1,0:T(8,128)S(1)} %copy-done.8), channel_id=1, replica_groups=mesh['groups'=2,'chan'=8,'sub'=2] {'chan'}, dimensions={0}, use_global_device_ids=true | all-gather | bytes 142848 | tf_op jit(solution)/shard_map/all_gather | solution.py:180
  44.9 225.0 %while.12 = (s32[]{:T(128)}, f32[32,62,128]{2,1,0:T(8,128)S(1)}, f32[32,62,16]{1,2,0:T(8,128)S(1)}, s32[16,32]{1,0:T(8,128)S(1)}, s32[16,32]{1,0:T(8,128)S(1)}, ...) while((s32[]{:T(128)}, f32[32,62,128]{2,1,0:T(8,128)S(1)}, ...), condition=%wide.region_5.6_spmd, body=%wide.region_0.5_spmd.sunk | while | flops 259593408 | bytes 28256220 | solution.py:115
  49.5 1.8 scatter_fusion.1
  51.7 1.3 copy.192
  54.8 2.0 fusion.100
  56.8 2.1 scatter_fusion
  63.5 1.8 scatter_fusion.1
  65.7 1.3 copy.192
  68.8 2.0 fusion.100
  70.8 2.1 scatter_fusion
  77.6 1.7 scatter_fusion.1
  79.8 1.3 copy.192
  82.9 2.0 fusion.100
  84.9 2.1 scatter_fusion
  91.7 1.7 scatter_fusion.1
  93.8 1.3 copy.192
  96.9 2.0 fusion.100
  98.9 2.1 scatter_fusion
  105.7 1.7 scatter_fusion.1
  107.9 1.3 copy.192
  111.0 2.0 fusion.100
  113.0 2.1 scatter_fusion
  119.8 1.8 scatter_fusion.1
  122.0 1.3 copy.192
  125.1 2.0 fusion.100
  127.1 2.1 scatter_fusion
  133.8 1.7 scatter_fusion.1
  136.0 1.3 copy.192
  139.1 2.0 fusion.100
  141.1 2.1 scatter_fusion
  147.9 1.7 scatter_fusion.1
  153.2 2.0 fusion.100
  155.2 2.1 scatter_fusion
  161.9 1.7 scatter_fusion.1
  167.2 2.0 fusion.100
  169.2 2.1 scatter_fusion
  176.0 1.8 scatter_fusion.1
  181.3 2.0 fusion.100
  183.3 2.1 scatter_fusion
  190.1 1.8 scatter_fusion.1
  195.4 2.0 fusion.100
  197.4 2.1 scatter_fusion
  204.1 1.7 scatter_fusion.1
  209.4 2.0 fusion.100
  211.4 2.1 scatter_fusion
  218.2 1.7 scatter_fusion.1
  223.5 2.0 fusion.100
  225.5 2.1 scatter_fusion
  232.2 1.8 scatter_fusion.1
  237.5 2.0 fusion.100
  239.5 2.1 scatter_fusion
  246.3 1.8 scatter_fusion.1
  251.6 2.0 fusion.100
  253.6 2.1 scatter_fusion
  260.4 1.7 scatter_fusion.1
  265.7 2.0 fusion.100
  267.7 2.1 scatter_fusion
  270.6 2.0 copy.114
  275.2 52.2 %reduce-scatter.5.cloned.1.call-done = f32[2,62,16]{1,2,0:T(8,128)} async-done(((f32[32,62,16]{1,2,0:T(8,128)}), f32[2,62,16]{1,2,0:T(8,128)}) %reduce-scatter.5.cloned.1.call-update) | async-done | bytes 7952 | tf_op jit(solution)/shard_map/reduce_scatter | solution.py:193
  328.5 63.5 %reduce-scatter.3.cloned.1.call-done = f32[2,62,128]{1,2,0:T(8,128)} async-done(((f32[32,62,128]{1,2,0:T(8,128)}), f32[2,62,128]{1,2,0:T(8,128)}) %reduce-scatter.3.cloned.1.call-update) | async-done | bytes 63504 | tf_op jit(solution)/shard_map/reduce_scatter | solution.py:192
  394.5 181.8 %custom-call.21 = f32[2,62,16,16]{3,2,1,0:T(8,128)S(1)} custom-call(f32[2,62,16,16]{3,2,1,0:T(8,128)S(1)} %broadcast_multiply_fusion), custom_call_target="Cholesky" | custom-call | tf_op jit(solution)/shard_map/jit(cholesky)/cholesky | solution.py:139
  577.0 5.4 custom-call.22
  582.9 20.7 %all-gather = f32[64,2,62,8]{2,3,1,0:T(8,128)S(1)} all-gather(f32[4,2,62,8]{2,3,1,0:T(8,128)S(1)} %copy.126), channel_id=2, replica_groups=mesh['groups'=2,'chan'=8,'sub'=2] {'chan','sub'}, dimensions={0}, use_global_device_ids=true | all-gather | bytes 269824 | tf_op jit(solution)/shard_map/all_gather | solution.py:206
  (599 shorter events, 130.8 us)
Async XLA Ops:
  7.2 320.9 %copy-start = (f32[4,2,62,8]{2,3,1,0:T(8,128)S(1)}, f32[4,2,62,8]{2,3,1,0:T(8,128)}, u32[]{:S(2)}) copy-start(f32[4,2,62,8]{2,3,1,0:T(8,128)} %param.22) | copy-start | bytes 47620
  7.2 320.2 %reduce-scatter.5.cloned.1.call-start = ((), (), s32[]{:S(2)}) async-start(), calls=%async_computation.3 | async-start | bytes 278528 | tf_op jit(solution)/shard_map/reduce_scatter | solution.py:193
  8.2 3.7 copy-start.7
  8.2 3.7 copy-start.8
  8.2 36.3 %copy-start.11 = (s32[512,1]{0,1:T(1,128)S(1)}, s32[512,1]{0,1:T(1,128)}, u32[]{:S(2)}) copy-start(s32[512,1]{0,1:T(1,128)} %param.16) | copy-start | bytes 6148
  8.3 36.3 %copy-start.9 = (s32[512]{0:T(512)S(1)}, s32[512]{0:T(512)}, u32[]{:S(2)}) copy-start(s32[512]{0:T(512)} %param.17) | copy-start | bytes 6148
  8.3 36.4 %copy-start.10 = (s32[512]{0:T(512)S(1)}, s32[512]{0:T(512)}, u32[]{:S(2)}) copy-start(s32[512]{0:T(512)} %param.18) | copy-start | bytes 6148
  11.9 33.0 %copy-start.4 = (s32[15,2,128]{2,1,0:T(2,128)S(1)}, s32[15,2,128]{2,1,0:T(2,128)}, u32[]{:S(2)}) copy-start(s32[15,2,128]{2,1,0:T(2,128)} %param.19) | copy-start | bytes 46084
  44.9 3.7 copy-start.5
  49.1 2.1 copy-start.2
  53.3 1.5 copy-start.3
  56.8 2.2 copy-start.6
  58.9 3.7 copy-start.5
  63.2 2.1 copy-start.2
  70.8 2.2 copy-start.6
  73.0 3.7 copy-start.5
  77.2 2.1 copy-start.2
  84.9 2.1 copy-start.6
  87.0 3.7 copy-start.5
  91.3 2.1 copy-start.2
  98.9 2.1 copy-start.6
  101.1 3.7 copy-start.5
  105.3 2.1 copy-start.2
  109.5 1.5 copy-start.3
  113.0 2.2 copy-start.6
  115.2 3.7 copy-start.5
  119.4 2.1 copy-start.2
  123.6 1.5 copy-start.3
  127.0 2.2 copy-start.6
  129.2 3.7 copy-start.5
  133.5 2.1 copy-start.2
  141.1 2.2 copy-start.6
  143.3 3.7 copy-start.5
  147.5 2.1 copy-start.2
  155.2 2.2 copy-start.6
  157.3 3.7 copy-start.5
  161.6 2.1 copy-start.2
  169.2 2.2 copy-start.6
  171.4 3.7 copy-start.5
  175.6 2.1 copy-start.2
  179.8 1.5 copy-start.3
  183.3 2.2 copy-start.6
  185.5 3.7 copy-start.5
  189.7 2.1 copy-start.2
  197.3 2.2 copy-start.6
  199.5 3.7 copy-start.5
  203.8 2.1 copy-start.2
  211.4 2.2 copy-start.6
  213.6 3.7 copy-start.5
  217.8 2.1 copy-start.2
  225.5 2.1 copy-start.6
  227.6 3.7 copy-start.5
  231.9 2.1 copy-start.2
  239.5 2.2 copy-start.6
  241.7 3.7 copy-start.5
  245.9 2.1 copy-start.2
  253.6 2.2 copy-start.6
  255.8 3.7 copy-start.5
  260.0 2.1 copy-start.2
  264.2 1.5 copy-start.3
  267.7 2.2 copy-start.6
  270.6 121.4 %reduce-scatter.3.cloned.1.call-start = ((), (), s32[]{:S(2)}) async-start(), calls=%async_computation.2 | async-start | bytes 2228224 | tf_op jit(solution)/shard_map/reduce_scatter | solution.py:192
  270.6 4.5 copy-start.12
  270.6 57.5 %copy-start.13 = (f32[2,2,62,8]{2,3,1,0:T(8,128)S(1)}, f32[2,2,62,8]{2,3,1,0:T(8,128)}, u32[]{:S(2)}) copy-start(f32[2,2,62,8]{2,3,1,0:T(8,128)} %param.21) | copy-start | bytes 23812
  (12 other events, 16.7 us)
Sparse Core Ops, SparseCore 0:
  270.7 56.6 reduce-scatter.4
  331.1 60.8 reduce-scatter.2
